TPU v7x, 32 devices: a whole 2x2x4 slice. The times are simulated.
32 devices in a mesh: dp: 16 (over z, y, x), mp: 2 (over core).
Axes of the slice: x: 2, y: 2, z: 4, core: 2. Of those that a mesh axis runs over, the one named last changes fastest.
Arguments:
- normed: bfloat16 [6144, 2048], P(('dp', 'mp')), may hold values from -12 to 12
- key_grad: bfloat16 [6144, 512], P('dp', 'mp'), may hold values from -0.078125 to 0.078125
- stale: bfloat16 [16, 2048, 512], P('dp', None, 'mp'), may hold values from -1.5 to 1.5
- worker_flag: int32 [16], P('dp'), may hold values 0 or 1
- block_mask: int32 [16, 4], P('dp'), may hold values 0 or 1
- aggregate: float32 [2048, 512], P('dp', 'mp'), may hold values from -6 to 6
- master: float32 [2048, 512], P('dp', 'mp'), may hold values from -0.125 to 0.125
- moment_one: float32 [2048, 512], P('dp', 'mp'), may hold values from -6 to 6
- moment_two: float32 [2048, 512], P('dp', 'mp'), may hold values from 0.5 to 4
Outputs:
- new_aggregate: float32 [2048, 512], P('dp', 'mp')
- new_master: float32 [2048, 512], P('dp', 'mp')
- new_moment_one: float32 [2048, 512], P('dp', 'mp')
- new_moment_two: float32 [2048, 512], P('dp', 'mp')
- weights: bfloat16 [2048, 512], P(None, 'mp')
- new_stale: bfloat16 [16, 2048, 512], P('dp', None, 'mp')
All inputs are finite; a program needn't handle non-finite values. No bound on the sum of `worker_flag` on one device may be relied on, other than what follows from the above.
Results may differ from a plain program's by a relative error of at most 0.0004.
Values may be sent and summed in bfloat16 or wider, within the bound.
A program may use at most 64 MiB of HBM per device.

v0:
```python
import jax
import jax.numpy as jnp
from jax import lax
from jax.sharding import PartitionSpec as P

H = 512
BLOCKS = 4
STEP = 10


beta_one = 0.9
beta_two = 0.95
learn_rate = 0.001
decay_rate = 0.1
epsilon = 1e-08


def on_device(
    normed, key_grad, stale, worker_flag, block_mask, aggregate, master, moment_one, moment_two
):
    half_cols = key_grad.shape[1]
    first_col = lax.axis_index("mp") * half_cols
    columns = first_col + jnp.arange(half_cols, dtype=jnp.int32)
    column_block = columns // (H // BLOCKS)
    onehot = (column_block[:, None] == jnp.arange(BLOCKS, dtype=jnp.int32)[None, :]).astype(
        jnp.int32
    )
    trig = worker_flag[0] * jnp.sum(onehot * block_mask[0][None, :], axis=1)
    weight = trig.astype(jnp.float32)
    gathered = lax.all_gather(normed, "mp", axis=0, tiled=True)
    grad = lax.dot_general(
        gathered, key_grad, (((0,), (0,)), ((), ())), preferred_element_type=jnp.float32
    )
    old = stale[0]
    reduced = lax.psum_scatter(
        weight[None, :] * (grad - old.astype(jnp.float32)), "dp", scatter_dimension=0, tiled=True
    )
    new_aggregate = aggregate + reduced
    new_moment_one = beta_one * moment_one + (1.0 - beta_one) * new_aggregate
    new_moment_two = beta_two * moment_two + (1.0 - beta_two) * new_aggregate * new_aggregate
    first_hat = new_moment_one / (1.0 - beta_one**STEP)
    second_hat = new_moment_two / (1.0 - beta_two**STEP)
    update = first_hat / (jnp.sqrt(second_hat) + epsilon)
    new_master = master - learn_rate * (update + decay_rate * master)
    fresh = new_master.astype(jnp.bfloat16)
    weights = lax.all_gather(fresh, "dp", axis=0, tiled=True)
    kept = jnp.where(trig[None, :] > 0, grad.astype(jnp.bfloat16), old)
    return (new_aggregate, new_master, new_moment_one, new_moment_two, weights, kept[None])


def solution(mesh):
    placed = (
        P(("dp", "mp"), None),
        P("dp", "mp"),
        P("dp", None, "mp"),
        P("dp"),
        P("dp", None),
        P("dp", "mp"),
        P("dp", "mp"),
        P("dp", "mp"),
        P("dp", "mp"),
    )
    return jax.shard_map(
        on_device,
        mesh=mesh,
        in_specs=placed,
        out_specs=(
            P("dp", "mp"),
            P("dp", "mp"),
            P("dp", "mp"),
            P("dp", "mp"),
            P(None, "mp"),
            P("dp", None, "mp"),
        ),
        check_vma=False,
    )
```

profile of v0, /device:TPU:0, one launch (start us, length us, event | category | flops | bytes accessed | tf_op | source)
XLA Modules:
  0.0 172.6 jit_solution(14911570751095203750)
XLA Ops:
  7.2 0.0 copy-start
  7.2 0.0 all-gather.3.cloned.1.call-start
  7.2 0.7 all-gather.3.cloned.1.call-update
  7.9 0.0 reduce-scatter.2.cloned.1.call-start
  8.6 0.7 select_reduce_fusion
  9.4 12.7 %all-gather.3.cloned.1.call-done = bf16[384,2048]{1,0:T(8,128)(2,1)} async-done(((bf16[192,2048]{1,0:T(8,128)(2,1)}), bf16[384,2048]{1,0:T(8,128)(2,1)}) %all-gather.3.cloned.1.call-update) | async-done | bytes 1572880 | tf_op jit(solution)/shard_map/all_gather | solution.py:30
  22.1 0.0 copy-done
  22.1 3.8 %subtract_multiply_fusion = (f32[2048,256]{1,0:T(8,128)}, bf16[2048,256]{1,0:T(8,128)(2,1)S(1)}) fusion(bf16[1,2048,256]{2,1,0:T(8,128)(2,1)} %param.11, f32[256]{0:T(256)S(1)} %multiply_convert_fusion, bf16[384,2048]{1,0:T(8,128)(2,1)} %all-gather.3.cloned.1.call-done, bf16[384,256]{1,0:T(8,128)(2,1)S(1)} %copy-done), kind=kOutput, calls=%fused_computation | convolution fusion | flops 404750336 | bytes 5964800 | tf_op jit(solution)/shard_map/dot_general | solution.py:31
  25.9 0.0 copy-start.2
  25.9 0.0 copy-start.3
  25.9 0.0 copy-start.1
  25.9 0.0 reduce-scatter.2.cloned.1.call-update
  25.9 0.0 all-gather.5.cloned.1.call-start
  26.0 82.7 %reduce-scatter.2.cloned.1.call-done = f32[128,256]{1,0:T(8,128)} async-done(((f32[2048,256]{1,0:T(8,128)}), f32[128,256]{1,0:T(8,128)}) %reduce-scatter.2.cloned.1.call-update) | async-done | bytes 131088 | tf_op jit(solution)/shard_map/reduce_scatter | solution.py:35
  108.6 0.0 copy-done.2
  108.6 0.0 copy-done.3
  108.6 0.0 copy-done.4
  108.6 0.0 copy-done.5
  108.7 1.7 %fusion.2 = (bf16[128,256]{1,0:T(8,128)(2,1)}, f32[128,256]{1,0:T(8,128)}, f32[128,256]{1,0:T(8,128)}, f32[128,256]{1,0:T(8,128)}, f32[128,256]{1,0:T(8,128)}) fusion(f32[128,256]{1,0:T(8,128)S(1)} %copy-done.2, f32[128,256]{1,0:T(8,128)S(1)} %copy-done.3, f32[128,256]{1,0:T(8,128)S(1)} %copy-done.4, f32[128,256]{1,0:T(8,128)S(1)} %copy-done.5, ...), kind=kLoop, calls=%fused_computation.15 | loop fusion | flops 557056 | bytes 1245184 | tf_op jit(solution)/shard_map/convert_element_type | solution.py:45
  110.4 0.0 all-gather.5.cloned.1.call-update
  110.4 0.0 copy-done.1
  110.4 1.1 fusion
  111.5 52.3 %all-gather.5.cloned.1.call-done = bf16[2048,256]{1,0:T(8,128)(2,1)} async-done(((bf16[128,256]{1,0:T(8,128)(2,1)}), bf16[2048,256]{1,0:T(8,128)(2,1)}) %all-gather.5.cloned.1.call-update) | async-done | bytes 1048592 | tf_op jit(solution)/shard_map/all_gather | solution.py:46
  163.8 2.3 %copy.17 = bf16[2048,256]{1,0:T(8,128)(2,1)} copy(bf16[2048,256]{1,0:T(8,128)(2,1)} %all-gather.5.cloned.1.call-done) | data formatting | bytes 2097152
  (5 shorter events, 0.0 us)
Async XLA Ops:
  7.2 14.9 %copy-start = (bf16[384,256]{1,0:T(8,128)(2,1)S(1)}, bf16[384,256]{1,0:T(8,128)(2,1)}, u32[]{:S(2)}) copy-start(bf16[384,256]{1,0:T(8,128)(2,1)} %param.10) | copy-start | bytes 589828
  7.2 14.9 %all-gather.3.cloned.1.call-start = ((), (), s32[]{:S(2)}) async-start(), calls=%async_computation.1 | async-start | bytes 2359296 | tf_op jit(solution)/shard_map/all_gather | solution.py:30
  7.9 100.7 %reduce-scatter.2.cloned.1.call-start = ((), (), s32[]{:S(2)}) async-start(), calls=%async_computation.2 | async-start | bytes 2228224 | tf_op jit(solution)/shard_map/reduce_scatter | solution.py:35
  25.9 82.8 %copy-start.2 = (f32[128,256]{1,0:T(8,128)S(1)}, f32[128,256]{1,0:T(8,128)}, u32[]{:S(2)}) copy-start(f32[128,256]{1,0:T(8,128)} %param.15) | copy-start | bytes 393220
  25.9 82.8 %copy-start.3 = (f32[128,256]{1,0:T(8,128)S(1)}, f32[128,256]{1,0:T(8,128)}, u32[]{:S(2)}) copy-start(f32[128,256]{1,0:T(8,128)} %param.16) | copy-start | bytes 393220
  25.9 82.8 %copy-start.4 = (f32[128,256]{1,0:T(8,128)S(1)}, f32[128,256]{1,0:T(8,128)}, u32[]{:S(2)}) copy-start(f32[128,256]{1,0:T(8,128)} %param.17) | copy-start | bytes 393220
  25.9 82.8 %copy-start.5 = (f32[128,256]{1,0:T(8,128)S(1)}, f32[128,256]{1,0:T(8,128)}, u32[]{:S(2)}) copy-start(f32[128,256]{1,0:T(8,128)} %param.14) | copy-start | bytes 393220
  25.9 84.6 %copy-start.1 = (bf16[1,2048,256]{2,1,0:T(8,128)(2,1)S(1)}, bf16[1,2048,256]{2,1,0:T(8,128)(2,1)}, u32[]{:S(2)}) copy-start(bf16[1,2048,256]{2,1,0:T(8,128)(2,1)} %param.11) | copy-start | bytes 3145732
  25.9 137.9 %all-gather.5.cloned.1.call-start = ((), (), s32[]{:S(2)}) async-start(), calls=%async_computation.3 | async-start | bytes 1114112 | tf_op jit(solution)/shard_map/all_gather | solution.py:46
Sparse Core Ops, SparseCore 0:
  9.5 12.5 all-gather.2
  26.0 82.5 reduce-scatter.1
  112.0 51.8 all-gather.4
where the time goes:
time: 173 us
  waiting for transfers between devices  148 us (86%)
  between operations  14.4 us (8%)
  matrix products  3.78 us (2%)
  other arithmetic  3.59 us (2%)
  local copies, waits for them, and re-layouts  2.29 us (1%)
    reduce_scatter x1, waiting for transfers between devices, on_device(): lax.psum_scatter(weight[None, :] * (grad - old.astype(jnp.float32)), 'dp'...  82.7 us
    all_gather x1, waiting for transfers between devices, on_device(): weights = lax.all_gather(fresh, 'dp', axis=0, tiled=True)  52.3 us
    all_gather x1, waiting for transfers between devices, on_device(): gathered = lax.all_gather(normed, 'mp', axis=0, tiled=True)  12.7 us
    dot_general x1, matrix products, on_device(): lax.dot_general(gathered, key_grad, (((0,), (0,)), ((), ())), preferred_e...  3.78 us
  transfers between devices with their start and end apart: 3, of which 3 were waited for; matrix products, arithmetic and copies ran while one was open for 1% of the time, Pallas kernels for 0%

commit v1 on v0

v1 whole, which is shorter than its diff:
```python
import functools
import math

import jax
import jax.numpy as jnp
from jax import lax
from jax.experimental import pallas as pl
from jax.experimental.pallas import tpu as pltpu
from jax.sharding import PartitionSpec as P

H = 512
BLOCKS = 4
STEP = 10


beta_one = 0.9
beta_two = 0.95
learn_rate = 0.001
decay_rate = 0.1
epsilon = 1e-08

LANES = 128
WIRE = jnp.float32
MESH = pl.DeviceIdType.MESH


def grid_of(workers):
    inner = max(i for i in range(1, math.isqrt(workers // 2) + 1) if workers % (i * i) == 0)
    return workers // (inner * inner), inner


def encode(values):
    return values


def decode(values):
    return values


def kernel(
    zs, ins, mps, width,
    normed, key_grad, stale, flag, mask, aggregate, master, moment_one, moment_two,
    out_aggregate, out_master, out_one, out_two, out_weights, out_stale,
    mine, theirs, kgrad, old, kept, states,
    part, wire, got_one, sum_one, wire_two, got_two, wire_three, own_sum, got_three,
    load_sem, store_sem, mp_send, mp_recv, one_send, one_recv, two_send, two_recv,
    three_send, three_recv, gz_send, gz_recv, gs_send, gs_recv, gl_send, gl_recv,
):
    me = lax.axis_index("dp")
    core = lax.axis_index("mp")
    z, a, b = me // (ins * ins), lax.rem(me // ins, ins), lax.rem(me, ins)
    tokens = normed.shape[0]
    slab = normed.shape[1] // zs
    rows = slab // (ins * ins)
    cols = key_grad.shape[1]

    def at(zz, aa, bb):
        return {"dp": (zz * ins + aa) * ins + bb}

    def hop(base, j, size):
        return lax.rem(base + j, size)

    loads = [
        pltpu.make_async_copy(src, dst, load_sem.at[i])
        for i, (src, dst) in enumerate(
            [(normed, mine), (key_grad, kgrad), (stale.at[0], old)]
            + [(src, states.at[i]) for i, src in enumerate((aggregate, master, moment_one, moment_two))]
        )
    ]
    for load in loads:
        load.start()

    peers = [{"mp": hop(core, j, mps)} for j in range(1, mps)]
    peers += [at(hop(z, j, zs), a, b) for j in range(1, zs)]
    peers += [at(z, hop(a, j, ins), b) for j in range(1, ins)]
    peers += [at(z, a, hop(b, j, ins)) for j in range(1, ins)]
    barrier = pltpu.get_barrier_semaphore()
    for peer in peers:
        pl.semaphore_signal(barrier, inc=1, device_id=peer, device_id_type=MESH)
    pl.semaphore_wait(barrier, len(peers))

    pending = []

    def send(src, dst, send_sem, recv_sem, peer):
        copy = pltpu.make_async_remote_copy(
            src_ref=src, dst_ref=dst, send_sem=send_sem, recv_sem=recv_sem,
            device_id=peer, device_id_type=MESH,
        )
        copy.start()
        pending.append(copy)
        return copy

    order = list(range(1, zs)) + [0]
    shared = {}
    for k in order:
        columns = pl.ds(pl.multiple_of(hop(z, k, zs) * slab, slab), slab)
        shared[k] = [
            send(
                normed.at[:, columns], theirs.at[j - 1, :, columns],
                mp_send.at[k, j - 1], mp_recv.at[k, j - 1], {"mp": hop(core, j, mps)},
            )
            for j in range(1, mps)
        ]

    block = (core * cols + lax.broadcasted_iota(jnp.int32, (1, cols), 1)) // width
    trig = jnp.zeros((1, cols), jnp.int32)
    for i in range(BLOCKS):
        trig = trig + jnp.where(block == i, flag[0] * mask[0, i], 0)
    weight = trig.astype(jnp.float32)

    for load in loads[:3]:
        load.wait()

    stores = []

    def compute(k):
        base = pl.multiple_of(hop(z, k, zs) * slab, slab)
        columns = pl.ds(base, slab)

        def product(left, owner):
            held = kgrad[pl.ds(pl.multiple_of(owner * tokens, tokens), tokens), :]
            return lax.dot_general(
                left, held, (((0,), (0,)), ((), ())), preferred_element_type=jnp.float32
            )

        grad = product(mine[:, columns], core)
        for j in range(1, mps):
            shared[k][j - 1].wait_recv()
            grad = grad + product(theirs[j - 1, :, columns], hop(core, mps - j, mps))
        before = old[pl.ds(base, slab), :].astype(jnp.float32)
        kept[pl.ds(base, slab), :] = jnp.where(trig > 0, grad, before).astype(jnp.bfloat16)
        change = weight * (grad - before)
        for s in range(2):
            piece = change[:, s * LANES:(s + 1) * LANES].reshape(ins, ins, rows, LANES)
            part[s, k] = piece
            if WIRE != jnp.float32:
                wire[s, k] = encode(piece)
        store = pltpu.make_async_copy(
            kept.at[pl.ds(base, slab), :], out_stale.at[0, pl.ds(base, slab), :], store_sem.at[k]
        )
        store.start()
        stores.append(store)

    firsts, seconds, thirds = {}, {}, {}
    source = part if WIRE == jnp.float32 else wire
    source_two = sum_one if WIRE == jnp.float32 else wire_two

    def send_one(k):
        firsts[k] = []
        for j in range(1, ins):
            bb, aa = hop(b, j, ins), hop(a, j, ins)
            firsts[k].append((
                send(source.at[0, k, :, bb], got_one.at[0, k, j - 1],
                     one_send.at[0, k, j - 1], one_recv.at[0, k, j - 1], at(z, a, bb)),
                send(source.at[1, k, aa], got_one.at[1, k, j - 1],
                     one_send.at[1, k, j - 1], one_recv.at[1, k, j - 1], at(z, aa, b)),
            ))

    def send_two(k):
        for s in range(2):
            total = part[0, k, :, b] if s == 0 else part[1, k, a]
            for j in range(1, ins):
                firsts[k][j - 1][s].wait_recv()
                total = total + decode(got_one[s, k, j - 1])
            sum_one[s, k] = total
            if WIRE != jnp.float32:
                wire_two[s, k] = encode(total)
        seconds[k] = []
        for j in range(1, ins):
            bb, aa = hop(b, j, ins), hop(a, j, ins)
            seconds[k].append((
                send(source_two.at[0, k, aa], got_two.at[0, k, j - 1],
                     two_send.at[0, k, j - 1], two_recv.at[0, k, j - 1], at(z, aa, b)),
                send(source_two.at[1, k, bb], got_two.at[1, k, j - 1],
                     two_send.at[1, k, j - 1], two_recv.at[1, k, j - 1], at(z, a, bb)),
            ))

    def send_three(k):
        for s in range(2):
            total = sum_one[s, k, a if s == 0 else b]
            for j in range(1, ins):
                seconds[k][j - 1][s].wait_recv()
                total = total + decode(got_two[s, k, j - 1])
            if k == 0:
                own_sum[s] = total
            else:
                wire_three[k - 1, s] = encode(total)
        if k:
            thirds[k] = send(wire_three.at[k - 1], got_three.at[k - 1],
                             three_send.at[k - 1], three_recv.at[k - 1], at(hop(z, k, zs), a, b))

    compute(order[0])
    send_one(order[0])
    for i in range(1, zs + 2):
        if i < zs:
            compute(order[i])
            send_one(order[i])
        if 0 <= i - 1 < zs:
            send_two(order[i - 1])
        if 0 <= i - 2 < zs:
            send_three(order[i - 2])

    for load in loads[3:]:
        load.wait()
    for k in range(1, zs):
        thirds[k].wait_recv()
    for s in range(2):
        here = pl.ds(s * LANES, LANES)
        total = own_sum[s]
        for k in range(1, zs):
            total = total + decode(got_three[k - 1, s])
        new_aggregate = states[0, :, here] + total
        out_aggregate[:, here] = new_aggregate
        new_one = beta_one * states[2, :, here] + (1.0 - beta_one) * new_aggregate
        new_two = beta_two * states[3, :, here] + (1.0 - beta_two) * new_aggregate * new_aggregate
        out_one[:, here] = new_one
        out_two[:, here] = new_two
        first_hat = new_one / (1.0 - beta_one**STEP)
        second_hat = new_two / (1.0 - beta_two**STEP)
        update = first_hat / (jnp.sqrt(second_hat) + epsilon)
        held = states[1, :, here]
        new_master = held - learn_rate * (update + decay_rate * held)
        out_master[:, here] = new_master
        out_weights[z, a, b, :, here] = new_master.astype(jnp.bfloat16)

    halves = [pl.ds(s * LANES, LANES) for s in range(2)]
    spread = {
        k: send(out_weights.at[z, a, b], out_weights.at[z, a, b],
                gz_send.at[k - 1], gz_recv.at[k - 1], at(hop(z, k, zs), a, b))
        for k in range(1, zs)
    }
    shorts, longs = {}, {}

    def gather_short(k):
        zz = hop(z, zs - k, zs)
        if k:
            spread[k].wait_recv()
        shorts[k] = []
        for j in range(1, ins):
            bb, aa = hop(b, j, ins), hop(a, j, ins)
            for s, peer in ((0, at(z, aa, b)), (1, at(z, a, bb))):
                ref = out_weights.at[zz, a, b, :, halves[s]]
                shorts[k].append(
                    send(ref, ref, gs_send.at[s, k, j - 1], gs_recv.at[s, k, j - 1], peer)
                )

    def gather_long(k):
        zz = hop(z, zs - k, zs)
        for copy in shorts[k]:
            copy.wait_recv()
        longs[k] = []
        for j in range(1, ins):
            bb, aa = hop(b, j, ins), hop(a, j, ins)
            for s, peer in ((0, at(z, a, bb)), (1, at(z, aa, b))):
                ref = (out_weights.at[zz, :, b, :, halves[0]] if s == 0
                       else out_weights.at[zz, a, :, :, halves[1]])
                longs[k].append(
                    send(ref, ref, gl_send.at[s, k, j - 1], gl_recv.at[s, k, j - 1], peer)
                )

    turn = list(range(zs))
    for i in range(zs + 1):
        if i < zs:
            gather_short(turn[i])
        if i >= 1:
            gather_long(turn[i - 1])
    for k in turn:
        for copy in longs[k]:
            copy.wait_recv()
    for copy in pending:
        copy.wait_send()
    for store in stores:
        store.wait()


def on_device(
    workers, mps,
    normed, key_grad, stale, worker_flag, block_mask, aggregate, master, moment_one, moment_two
):
    zs, ins = grid_of(workers)
    tokens, depth = normed.shape
    cols = key_grad.shape[1]
    rows = aggregate.shape[0]
    f32, bf16 = jnp.float32, jnp.bfloat16
    dma = pltpu.SemaphoreType.DMA
    anywhere = pl.BlockSpec(memory_space=pl.ANY)
    vmem = pl.BlockSpec(memory_space=pltpu.VMEM)
    smem = pl.BlockSpec(memory_space=pltpu.SMEM)
    state = jax.ShapeDtypeStruct((rows, cols), f32)
    one = (2, zs, ins, ins, rows, LANES)
    two = (2, zs, ins, rows, LANES)
    coded = WIRE != f32
    tiny = (1, 1, 1, 1, 8, LANES)
    results = pl.pallas_call(
        functools.partial(kernel, zs, ins, mps, H // BLOCKS),
        out_shape=(
            state, state, state, state,
            jax.ShapeDtypeStruct((zs, ins, ins, rows, cols), bf16),
            jax.ShapeDtypeStruct(stale.shape, bf16),
        ),
        in_specs=[anywhere] * 3 + [smem] * 2 + [anywhere] * 4,
        out_specs=(vmem,) * 5 + (anywhere,),
        scratch_shapes=[
            pltpu.VMEM((tokens, depth), bf16),
            pltpu.VMEM((mps - 1, tokens, depth), bf16),
            pltpu.VMEM(key_grad.shape, bf16),
            pltpu.VMEM((depth, cols), bf16),
            pltpu.VMEM((depth, cols), bf16),
            pltpu.VMEM((4, rows, cols), f32),
            pltpu.VMEM(one, f32),
            pltpu.VMEM(one if coded else tiny, WIRE),
            pltpu.VMEM((2, zs, ins - 1, ins, rows, LANES), WIRE),
            pltpu.VMEM(two, f32),
            pltpu.VMEM(two if coded else tiny[1:], WIRE),
            pltpu.VMEM((2, zs, ins - 1, rows, LANES), WIRE),
            pltpu.VMEM((zs - 1, 2, rows, LANES), WIRE),
            pltpu.VMEM((2, rows, LANES), f32),
            pltpu.VMEM((zs - 1, 2, rows, LANES), WIRE),
            dma((7,)), dma((zs,)),
            dma((zs, mps - 1)), dma((zs, mps - 1)),
            dma((2, zs, ins - 1)), dma((2, zs, ins - 1)),
            dma((2, zs, ins - 1)), dma((2, zs, ins - 1)),
            dma((zs - 1,)), dma((zs - 1,)),
            dma((zs - 1,)), dma((zs - 1,)),
            dma((2, zs, ins - 1)), dma((2, zs, ins - 1)),
            dma((2, zs, ins - 1)), dma((2, zs, ins - 1)),
        ],
        compiler_params=pltpu.CompilerParams(
            collective_id=0, has_side_effects=True, vmem_limit_bytes=48 * 1024 * 1024
        ),
    )(normed, key_grad, stale, worker_flag, block_mask, aggregate, master, moment_one, moment_two)
    return results[:4] + (results[4].reshape(depth, cols), results[5])


def solution(mesh):
    placed = (
        P(("dp", "mp"), None),
        P("dp", "mp"),
        P("dp", None, "mp"),
        P("dp"),
        P("dp", None),
        P("dp", "mp"),
        P("dp", "mp"),
        P("dp", "mp"),
        P("dp", "mp"),
    )
    return jax.shard_map(
        functools.partial(on_device, mesh.shape["dp"], mesh.shape["mp"]),
        mesh=mesh,
        in_specs=placed,
        out_specs=(
            P("dp", "mp"),
            P("dp", "mp"),
            P("dp", "mp"),
            P("dp", "mp"),
            P(None, "mp"),
            P("dp", None, "mp"),
        ),
        check_vma=False,
    )
```

time: 173 us -> 62.4 us (0.36)
  waiting for transfers between devices: 148 us -> 0 us
  Pallas kernels: 0 us -> 49.3 us
  between operations: 14.4 us -> 1.33 us
  local copies, waits for them, and re-layouts: 2.29 us -> 11.5 us
  matrix products: 3.78 us -> 0 us
  other arithmetic: 3.59 us -> 0 us
    reduce_scatter x1 -> x0, waiting for transfers between devices: 82.7 us -> none  [on_device(): lax.psum_scatter(weight[None, :] * (grad - old.astype(jnp.float32)), 'dp'...]
    all_gather x2 -> x0, waiting for transfers between devices: 65 us -> none  [the longest x1 52.3 us: on_device(): weights = lax.all_gather(fresh, 'dp', axis=0, tiled=True)]
    pallas_call x0 -> x1, Pallas kernels: none -> 49.3 us  [on_device(): pl.pallas_call(functools.partial(kernel, zs, ins, mps, H // BLOCKS), out_...]
    unnamed x13 -> x22, local copies, waits for them, and re-layouts: 2.29 us -> 11.5 us
    dot_general x1 -> x0, matrix products: 3.78 us -> none  [on_device(): lax.dot_general(gathered, key_grad, (((0,), (0,)), ((), ())), preferred_e...]
    convert_element_type x2 -> x0, other arithmetic: 1.75 us -> none  [the longest x1 1.74 us: on_device(): fresh = new_master.astype(jnp.bfloat16)]
  transfers between devices with their start and end apart: 3 -> 0, of which waited for: 3 -> 0; matrix products, arithmetic and copies ran while one was open for 1% -> 0% of each run, Pallas kernels for 0% -> 0%
where the time goes in v1:
time: 62.4 us; the launch traced here: 62.1 us
  Pallas kernels  49.3 us (79%)
  local copies, waits for them, and re-layouts  11.5 us (18%)
  between operations  1.33 us (2%)
    pallas_call x1, Pallas kernels, on_device(): pl.pallas_call(functools.partial(kernel, zs, ins, mps, H // BLOCKS), out_...  49.3 us
    unnamed x22, local copies, waits for them, and re-layouts  11.5 us

profile of v1, /device:TPU:0, one launch (start us, length us, event | category | flops | bytes accessed | tf_op | source)
XLA Modules:
  0.0 62.1 jit_solution(12012038038845787900)
XLA Ops:
  0.6 0.0 copy-start.7
  1.3 0.0 copy-done.7
  1.3 0.0 copy-start
  1.3 1.2 %copy-done = bf16[1,2048,256]{2,1,0:T(8,128)(2,1)S(1)} copy-done((bf16[1,2048,256]{2,1,0:T(8,128)(2,1)S(1)}, bf16[1,2048,256]{2,1,0:T(8,128)(2,1)}, u32[]{:S(2)}) %copy-start) | copy-done | bytes 1048600
  2.5 0.0 copy-start.1
  2.5 1.1 %copy-done.1 = bf16[192,2048]{1,0:T(8,128)(2,1)S(1)} copy-done((bf16[192,2048]{1,0:T(8,128)(2,1)S(1)}, bf16[192,2048]{1,0:T(8,128)(2,1)}, u32[]{:S(2)}) %copy-start.1) | copy-done | bytes 786456
  3.7 0.0 copy-start.2
  3.7 0.9 %copy-done.2 = bf16[384,256]{1,0:T(8,128)(2,1)S(1)} copy-done((bf16[384,256]{1,0:T(8,128)(2,1)S(1)}, bf16[384,256]{1,0:T(8,128)(2,1)}, u32[]{:S(2)}) %copy-start.2) | copy-done | bytes 196632
  4.6 0.0 copy-start.3
  4.6 0.9 %copy-done.3 = f32[128,256]{1,0:T(8,128)S(1)} copy-done((f32[128,256]{1,0:T(8,128)S(1)}, f32[128,256]{1,0:T(8,128)}, u32[]{:S(2)}) %copy-start.3) | copy-done | bytes 131096
  5.5 0.0 copy-start.4
  5.5 0.9 %copy-done.4 = f32[128,256]{1,0:T(8,128)S(1)} copy-done((f32[128,256]{1,0:T(8,128)S(1)}, f32[128,256]{1,0:T(8,128)}, u32[]{:S(2)}) %copy-start.4) | copy-done | bytes 131096
  6.4 0.0 copy-start.5
  6.4 0.9 %copy-done.5 = f32[128,256]{1,0:T(8,128)S(1)} copy-done((f32[128,256]{1,0:T(8,128)S(1)}, f32[128,256]{1,0:T(8,128)}, u32[]{:S(2)}) %copy-start.5) | copy-done | bytes 131096
  7.3 0.0 copy-start.6
  7.3 0.9 %copy-done.6 = f32[128,256]{1,0:T(8,128)S(1)} copy-done((f32[128,256]{1,0:T(8,128)S(1)}, f32[128,256]{1,0:T(8,128)}, u32[]{:S(2)}) %copy-start.6) | copy-done | bytes 131096
  8.2 49.3 %shard_map.136 = (f32[128,256]{1,0:T(8,128)S(1)}, f32[128,256]{1,0:T(8,128)S(1)}, f32[128,256]{1,0:T(8,128)S(1)}, f32[128,256]{1,0:T(8,128)S(1)}, bf16[4,2,2,128...) custom-call(bf16[192,2048]{1,0:T(8,128)(2,1)S(1)} %copy-done.1, bf16[384,256]{1,0:T(8,128)(2,1)S(1)} %copy-done.2, ...), custom_call_target="tpu_custom_call" | custom-call | tf_op jit(solution)/shard_map/pallas_call | solution.py:294
  57.5 0.7 %copy.22 = f32[128,256]{1,0:T(8,128)} copy(f32[128,256]{1,0:T(8,128)S(1)} %get-tuple-element.24) | data formatting | bytes 262144
  58.2 0.7 %copy.23 = f32[128,256]{1,0:T(8,128)} copy(f32[128,256]{1,0:T(8,128)S(1)} %get-tuple-element.25) | data formatting | bytes 262144
  58.8 0.7 %copy.24 = f32[128,256]{1,0:T(8,128)} copy(f32[128,256]{1,0:T(8,128)S(1)} %get-tuple-element.26) | data formatting | bytes 262144
  59.5 0.7 %copy.25 = f32[128,256]{1,0:T(8,128)} copy(f32[128,256]{1,0:T(8,128)S(1)} %get-tuple-element.27) | data formatting | bytes 262144
  60.1 1.0 %copy.26 = bf16[2048,256]{1,0:T(8,128)(2,1)} copy(bf16[2048,256]{1,0:T(8,128)(2,1)S(1)} %bitcast.1) | data formatting | bytes 2097152
  61.1 1.0 %copy.27 = bf16[1,2048,256]{2,1,0:T(8,128)(2,1)} copy(bf16[1,2048,256]{2,1,0:T(8,128)(2,1)S(1)} %get-tuple-element.29) | data formatting | bytes 2097152
Async XLA Ops:
  0.6 0.7 %copy-start.7 = (s32[1,4]{1,0:T(1,128)S(1)}, s32[1,4]{1,0:T(1,128)}, u32[]{:S(2)}) copy-start(s32[1,4]{1,0:T(1,128)} %mask.1) | copy-start | bytes 52
  1.3 1.2 %copy-start = (bf16[1,2048,256]{2,1,0:T(8,128)(2,1)S(1)}, bf16[1,2048,256]{2,1,0:T(8,128)(2,1)}, u32[]{:S(2)}) copy-start(bf16[1,2048,256]{2,1,0:T(8,128)(2,1)} %stale.1) | copy-start | bytes 3145732
  2.5 1.1 %copy-start.1 = (bf16[192,2048]{1,0:T(8,128)(2,1)S(1)}, bf16[192,2048]{1,0:T(8,128)(2,1)}, u32[]{:S(2)}) copy-start(bf16[192,2048]{1,0:T(8,128)(2,1)} %normed.1) | copy-start | bytes 2359300
  3.7 0.9 %copy-start.2 = (bf16[384,256]{1,0:T(8,128)(2,1)S(1)}, bf16[384,256]{1,0:T(8,128)(2,1)}, u32[]{:S(2)}) copy-start(bf16[384,256]{1,0:T(8,128)(2,1)} %key_grad.1) | copy-start | bytes 589828
  4.6 0.9 %copy-start.3 = (f32[128,256]{1,0:T(8,128)S(1)}, f32[128,256]{1,0:T(8,128)}, u32[]{:S(2)}) copy-start(f32[128,256]{1,0:T(8,128)} %aggregate.1) | copy-start | bytes 393220
  5.5 0.9 %copy-start.4 = (f32[128,256]{1,0:T(8,128)S(1)}, f32[128,256]{1,0:T(8,128)}, u32[]{:S(2)}) copy-start(f32[128,256]{1,0:T(8,128)} %master.1) | copy-start | bytes 393220
  6.4 0.9 %copy-start.5 = (f32[128,256]{1,0:T(8,128)S(1)}, f32[128,256]{1,0:T(8,128)}, u32[]{:S(2)}) copy-start(f32[128,256]{1,0:T(8,128)} %moment_one.1) | copy-start | bytes 393220
  7.3 0.9 %copy-start.6 = (f32[128,256]{1,0:T(8,128)S(1)}, f32[128,256]{1,0:T(8,128)}, u32[]{:S(2)}) copy-start(f32[128,256]{1,0:T(8,128)} %moment_two.1) | copy-start | bytes 393220

commit v2 on v1

--- a/solution.py
+++ b/solution.py
@@ -20,7 +20,9 @@
 epsilon = 1e-08
 
 LANES = 128
-WIRE = jnp.float32
+WIRE = jnp.int16
+FINEST = 2.0**14
+LEVELS = 1092.0
 MESH = pl.DeviceIdType.MESH
 
 
@@ -30,20 +32,24 @@
 
 
 def encode(values):
-    return values
-
-
-def decode(values):
-    return values
+    size = jnp.log2(1.0 + jnp.abs(values) * FINEST)
+    code = jnp.minimum(size * LEVELS + 0.5, 32767.0).astype(jnp.int32)
+    return jnp.where(values < 0, -code, code).astype(jnp.int16)
+
+
+def decode(codes):
+    code = codes.astype(jnp.int32).astype(jnp.float32)
+    size = (jnp.exp2(jnp.abs(code) * (1.0 / LEVELS)) - 1.0) * (1.0 / FINEST)
+    return jnp.where(code < 0, -size, size)
 
 
 def kernel(
     zs, ins, mps, width,
     normed, key_grad, stale, flag, mask, aggregate, master, moment_one, moment_two,
-    out_aggregate, out_master, out_one, out_two, out_weights, out_stale,
-    mine, theirs, kgrad, old, kept, states,
+    out_aggregate, out_master, out_one, out_two, out_weights, kept,
+    mine, theirs, kgrad, old, states,
     part, wire, got_one, sum_one, wire_two, got_two, wire_three, own_sum, got_three,
-    load_sem, store_sem, mp_send, mp_recv, one_send, one_recv, two_send, two_recv,
+    load_sem, mp_send, mp_recv, one_send, one_recv, two_send, two_recv,
     three_send, three_recv, gz_send, gz_recv, gs_send, gs_recv, gl_send, gl_recv,
 ):
     me = lax.axis_index("dp")
@@ -110,8 +116,6 @@
 
     for load in loads[:3]:
         load.wait()
-
-    stores = []
 
     def compute(k):
         base = pl.multiple_of(hop(z, k, zs) * slab, slab)
@@ -135,11 +139,6 @@
             part[s, k] = piece
             if WIRE != jnp.float32:
                 wire[s, k] = encode(piece)
-        store = pltpu.make_async_copy(
-            kept.at[pl.ds(base, slab), :], out_stale.at[0, pl.ds(base, slab), :], store_sem.at[k]
-        )
-        store.start()
-        stores.append(store)
 
     firsts, seconds, thirds = {}, {}, {}
     source = part if WIRE == jnp.float32 else wire
@@ -269,8 +268,17 @@
             copy.wait_recv()
     for copy in pending:
         copy.wait_send()
-    for store in stores:
-        store.wait()
+
+
+def write_out(*refs):
+    copies = [
+        pltpu.make_async_copy(src, dst, refs[12].at[i])
+        for i, (src, dst) in enumerate(zip(refs[:6], refs[6:12]))
+    ]
+    for copy in reversed(copies):
+        copy.start()
+    for copy in copies:
+        copy.wait()
 
 
 def on_device(
@@ -283,8 +291,9 @@
     rows = aggregate.shape[0]
     f32, bf16 = jnp.float32, jnp.bfloat16
     dma = pltpu.SemaphoreType.DMA
-    anywhere = pl.BlockSpec(memory_space=pl.ANY)
+    hbm = pl.BlockSpec(memory_space=pltpu.HBM)
     vmem = pl.BlockSpec(memory_space=pltpu.VMEM)
+    far = functools.partial(pltpu.with_memory_space_constraint, memory_space=pltpu.HBM)
     smem = pl.BlockSpec(memory_space=pltpu.SMEM)
     state = jax.ShapeDtypeStruct((rows, cols), f32)
     one = (2, zs, ins, ins, rows, LANES)
@@ -296,15 +305,14 @@
         out_shape=(
             state, state, state, state,
             jax.ShapeDtypeStruct((zs, ins, ins, rows, cols), bf16),
-            jax.ShapeDtypeStruct(stale.shape, bf16),
+            jax.ShapeDtypeStruct((depth, cols), bf16),
         ),
-        in_specs=[anywhere] * 3 + [smem] * 2 + [anywhere] * 4,
-        out_specs=(vmem,) * 5 + (anywhere,),
+        in_specs=[hbm] * 3 + [smem] * 2 + [hbm] * 4,
+        out_specs=(vmem,) * 6,
         scratch_shapes=[
             pltpu.VMEM((tokens, depth), bf16),
             pltpu.VMEM((mps - 1, tokens, depth), bf16),
             pltpu.VMEM(key_grad.shape, bf16),
-            pltpu.VMEM((depth, cols), bf16),
             pltpu.VMEM((depth, cols), bf16),
             pltpu.VMEM((4, rows, cols), f32),
             pltpu.VMEM(one, f32),
@@ -316,7 +324,7 @@
             pltpu.VMEM((zs - 1, 2, rows, LANES), WIRE),
             pltpu.VMEM((2, rows, LANES), f32),
             pltpu.VMEM((zs - 1, 2, rows, LANES), WIRE),
-            dma((7,)), dma((zs,)),
+            dma((7,)),
             dma((zs, mps - 1)), dma((zs, mps - 1)),
             dma((2, zs, ins - 1)), dma((2, zs, ins - 1)),
             dma((2, zs, ins - 1)), dma((2, zs, ins - 1)),
@@ -328,8 +336,20 @@
         compiler_params=pltpu.CompilerParams(
             collective_id=0, has_side_effects=True, vmem_limit_bytes=48 * 1024 * 1024
         ),
-    )(normed, key_grad, stale, worker_flag, block_mask, aggregate, master, moment_one, moment_two)
-    return results[:4] + (results[4].reshape(depth, cols), results[5])
+    )(
+        far(normed), far(key_grad), far(stale), worker_flag, block_mask,
+        far(aggregate), far(master), far(moment_one), far(moment_two),
+    )
+    results = results[:4] + (results[4].reshape(depth, cols), results[5])
+    results = pl.pallas_call(
+        write_out,
+        out_shape=tuple(pltpu.HBM(x.shape, x.dtype) for x in results),
+        in_specs=[vmem] * 6,
+        out_specs=(hbm,) * 6,
+        scratch_shapes=[dma((6,))],
+        compiler_params=pltpu.CompilerParams(vmem_limit_bytes=2 * 1024 * 1024),
+    )(*results)
+    return results[:5] + (results[5][None],)
 
 
 def solution(mesh):

time: 62.4 us -> 42.9 us (0.69)
  local copies, waits for them, and re-layouts: 11.5 us -> 0.01 us
  Pallas kernels: 49.3 us -> 41.4 us
    unnamed x22 -> x2, local copies, waits for them, and re-layouts: 11.5 us -> 0.01 us
    pallas_call x1, Pallas kernels: 49.3 us -> 39.9 us  [on_device(): pl.pallas_call(functools.partial(kernel, zs, ins, mps, H // BLOCKS), out_...]
    pallas_call x0 -> x1, Pallas kernels: none -> 1.54 us  [on_device(): pl.pallas_call(write_out, out_shape=tuple((pltpu.HBM(x.shape, x.dtype) fo...]
where the time goes in v2:
time: 42.9 us; the launch traced here: 42.7 us
  Pallas kernels  41.4 us (97%)
  between operations  1.32 us (3%)
    pallas_call x1, Pallas kernels, on_device(): pl.pallas_call(functools.partial(kernel, zs, ins, mps, H // BLOCKS), out_...  39.9 us
    pallas_call x1, Pallas kernels, on_device(): pl.pallas_call(write_out, out_shape=tuple((pltpu.HBM(x.shape, x.dtype) fo...  1.54 us

profile of v2, /device:TPU:0, one launch (start us, length us, event | category | flops | bytes accessed | tf_op | source)
XLA Modules:
  0.0 42.7 jit_solution(6955987525332584677)
XLA Ops:
  0.6 0.0 copy-start
  1.3 0.0 copy-done
  1.3 39.9 %shard_map.136 = (f32[128,256]{1,0:T(8,128)S(1)}, f32[128,256]{1,0:T(8,128)S(1)}, f32[128,256]{1,0:T(8,128)S(1)}, f32[128,256]{1,0:T(8,128)S(1)}, bf16[4,2,2,128...) custom-call(bf16[192,2048]{1,0:T(8,128)(2,1)} %normed.1, bf16[384,256]{1,0:T(8,128)(2,1)} %key_grad.1, ...), custom_call_target="tpu_custom_call" | custom-call | tf_op jit(solution)/shard_map/pallas_call | solution.py:303
  41.2 1.5 %shard_map.137 = (f32[128,256]{1,0:T(8,128)}, f32[128,256]{1,0:T(8,128)}, f32[128,256]{1,0:T(8,128)}, f32[128,256]{1,0:T(8,128)}, bf16[2048,256]{1,0:T(8,128)(2,1)}, /*index=5*/bf16[2048,256]{1,0:T(8,128)(2,1)}) custom-call(f32[128,256]{1,0:T(8,128)S(1)} %get-tuple-element.18.refs_0_, f32[128,256]{1,0:T(8,128)S(1)} %get-tuple-element.19.refs_1_, ...), custom_call_target="tpu_custom_call" | custom-call | tf_op jit(solution)/shard_map/pallas_call | solution.py:344
Async XLA Ops:
  0.6 0.7 %copy-start = (s32[1,4]{1,0:T(1,128)S(1)}, s32[1,4]{1,0:T(1,128)}, u32[]{:S(2)}) copy-start(s32[1,4]{1,0:T(1,128)} %mask.1) | copy-start | bytes 52

commit v3 on v2

--- a/solution.py
+++ b/solution.py
@@ -45,12 +45,13 @@
 
 def kernel(
     zs, ins, mps, width,
-    normed, key_grad, stale, flag, mask, aggregate, master, moment_one, moment_two,
+    normed, key_grad, stale, flag, far_mask, aggregate, master, moment_one, moment_two,
     out_aggregate, out_master, out_one, out_two, out_weights, kept,
     mine, theirs, kgrad, old, states,
     part, wire, got_one, sum_one, wire_two, got_two, wire_three, own_sum, got_three,
-    load_sem, mp_send, mp_recv, one_send, one_recv, two_send, two_recv,
+    mask, load_sem, mp_send, mp_recv, one_send, one_recv, two_send, two_recv,
     three_send, three_recv, gz_send, gz_recv, gs_send, gs_recv, gl_send, gl_recv,
+    gd_send, gd_recv,
 ):
     me = lax.axis_index("dp")
     core = lax.axis_index("mp")
@@ -69,7 +70,7 @@
     loads = [
         pltpu.make_async_copy(src, dst, load_sem.at[i])
         for i, (src, dst) in enumerate(
-            [(normed, mine), (key_grad, kgrad), (stale.at[0], old)]
+            [(far_mask, mask), (normed, mine), (key_grad, kgrad), (stale.at[0], old)]
             + [(src, states.at[i]) for i, src in enumerate((aggregate, master, moment_one, moment_two))]
         )
     ]
@@ -108,13 +109,14 @@
             for j in range(1, mps)
         ]
 
+    loads[0].wait()
     block = (core * cols + lax.broadcasted_iota(jnp.int32, (1, cols), 1)) // width
     trig = jnp.zeros((1, cols), jnp.int32)
     for i in range(BLOCKS):
         trig = trig + jnp.where(block == i, flag[0] * mask[0, i], 0)
     weight = trig.astype(jnp.float32)
 
-    for load in loads[:3]:
+    for load in loads[1:4]:
         load.wait()
 
     def compute(k):
@@ -137,8 +139,6 @@
         for s in range(2):
             piece = change[:, s * LANES:(s + 1) * LANES].reshape(ins, ins, rows, LANES)
             part[s, k] = piece
-            if WIRE != jnp.float32:
-                wire[s, k] = encode(piece)
 
     firsts, seconds, thirds = {}, {}, {}
     source = part if WIRE == jnp.float32 else wire
@@ -148,6 +148,9 @@
         firsts[k] = []
         for j in range(1, ins):
             bb, aa = hop(b, j, ins), hop(a, j, ins)
+            if WIRE != jnp.float32:
+                wire[0, k, :, bb] = encode(part[0, k, :, bb])
+                wire[1, k, aa] = encode(part[1, k, aa])
             firsts[k].append((
                 send(source.at[0, k, :, bb], got_one.at[0, k, j - 1],
                      one_send.at[0, k, j - 1], one_recv.at[0, k, j - 1], at(z, a, bb)),
@@ -162,11 +165,12 @@
                 firsts[k][j - 1][s].wait_recv()
                 total = total + decode(got_one[s, k, j - 1])
             sum_one[s, k] = total
-            if WIRE != jnp.float32:
-                wire_two[s, k] = encode(total)
         seconds[k] = []
         for j in range(1, ins):
             bb, aa = hop(b, j, ins), hop(a, j, ins)
+            if WIRE != jnp.float32:
+                wire_two[0, k, aa] = encode(sum_one[0, k, aa])
+                wire_two[1, k, bb] = encode(sum_one[1, k, bb])
             seconds[k].append((
                 send(source_two.at[0, k, aa], got_two.at[0, k, j - 1],
                      two_send.at[0, k, j - 1], two_recv.at[0, k, j - 1], at(z, aa, b)),
@@ -199,7 +203,7 @@
         if 0 <= i - 2 < zs:
             send_three(order[i - 2])
 
-    for load in loads[3:]:
+    for load in loads[4:]:
         load.wait()
     for k in range(1, zs):
         thirds[k].wait_recv()
@@ -228,13 +232,23 @@
                 gz_send.at[k - 1], gz_recv.at[k - 1], at(hop(z, k, zs), a, b))
         for k in range(1, zs)
     }
-    shorts, longs = {}, {}
+    shorts, longs, directs = {}, {}, {}
+
+    def gather_all(k, zz):
+        ref = out_weights.at[zz, a, b]
+        directs[k] = [
+            send(ref, ref, gd_send.at[k, j - 1], gd_recv.at[k, j - 1],
+                 at(z, hop(a, j // ins, ins), hop(b, j % ins, ins)))
+            for j in range(1, ins * ins)
+        ]
 
     def gather_short(k):
         zz = hop(z, zs - k, zs)
         if k:
             spread[k].wait_recv()
         shorts[k] = []
+        if k >= zs - 2:
+            return gather_all(k, zz)
         for j in range(1, ins):
             bb, aa = hop(b, j, ins), hop(a, j, ins)
             for s, peer in ((0, at(z, aa, b)), (1, at(z, a, bb))):
@@ -248,6 +262,8 @@
         for copy in shorts[k]:
             copy.wait_recv()
         longs[k] = []
+        if k >= zs - 2:
+            return
         for j in range(1, ins):
             bb, aa = hop(b, j, ins), hop(a, j, ins)
             for s, peer in ((0, at(z, a, bb)), (1, at(z, aa, b))):
@@ -264,7 +280,7 @@
         if i >= 1:
             gather_long(turn[i - 1])
     for k in turn:
-        for copy in longs[k]:
+        for copy in longs[k] + directs.get(k, []):
             copy.wait_recv()
     for copy in pending:
         copy.wait_send()
@@ -307,7 +323,7 @@
             jax.ShapeDtypeStruct((zs, ins, ins, rows, cols), bf16),
             jax.ShapeDtypeStruct((depth, cols), bf16),
         ),
-        in_specs=[hbm] * 3 + [smem] * 2 + [hbm] * 4,
+        in_specs=[hbm] * 3 + [smem] + [hbm] * 5,
         out_specs=(vmem,) * 6,
         scratch_shapes=[
             pltpu.VMEM((tokens, depth), bf16),
@@ -324,7 +340,8 @@
             pltpu.VMEM((zs - 1, 2, rows, LANES), WIRE),
             pltpu.VMEM((2, rows, LANES), f32),
             pltpu.VMEM((zs - 1, 2, rows, LANES), WIRE),
-            dma((7,)),
+            pltpu.SMEM(block_mask.shape, jnp.int32),
+            dma((8,)),
             dma((zs, mps - 1)), dma((zs, mps - 1)),
             dma((2, zs, ins - 1)), dma((2, zs, ins - 1)),
             dma((2, zs, ins - 1)), dma((2, zs, ins - 1)),
@@ -332,12 +349,13 @@
             dma((zs - 1,)), dma((zs - 1,)),
             dma((2, zs, ins - 1)), dma((2, zs, ins - 1)),
             dma((2, zs, ins - 1)), dma((2, zs, ins - 1)),
+            dma((zs, ins * ins - 1)), dma((zs, ins * ins - 1)),
         ],
         compiler_params=pltpu.CompilerParams(
             collective_id=0, has_side_effects=True, vmem_limit_bytes=48 * 1024 * 1024
         ),
     )(
-        far(normed), far(key_grad), far(stale), worker_flag, block_mask,
+        far(normed), far(key_grad), far(stale), worker_flag, far(block_mask),
         far(aggregate), far(master), far(moment_one), far(moment_two),
     )
     results = results[:4] + (results[4].reshape(depth, cols), results[5])

time: 42.9 us -> 41.2 us (0.960)
  Pallas kernels: 41.4 us -> 39.7 us
    pallas_call x1, Pallas kernels: 39.9 us -> 38.2 us  [on_device(): pl.pallas_call(functools.partial(kernel, zs, ins, mps, H // BLOCKS), out_...]
where the time goes in v3:
time: 41.2 us; the launch traced here: 41 us
  Pallas kernels  39.7 us (96%)
  between operations  1.29 us (3%)
    pallas_call x1, Pallas kernels, on_device(): pl.pallas_call(functools.partial(kernel, zs, ins, mps, H // BLOCKS), out_...  38.2 us
    pallas_call x1, Pallas kernels, on_device(): pl.pallas_call(write_out, out_shape=tuple((pltpu.HBM(x.shape, x.dtype) fo...  1.54 us

profile of v3, /device:TPU:0, one launch (start us, length us, event | category | flops | bytes accessed | tf_op | source)
XLA Modules:
  0.0 41.0 jit_solution(15964786131644013481)
XLA Ops:
  1.3 38.2 %shard_map.136 = (f32[128,256]{1,0:T(8,128)S(1)}, f32[128,256]{1,0:T(8,128)S(1)}, f32[128,256]{1,0:T(8,128)S(1)}, f32[128,256]{1,0:T(8,128)S(1)}, bf16[4,2,2,128...) custom-call(bf16[192,2048]{1,0:T(8,128)(2,1)} %normed.1, bf16[384,256]{1,0:T(8,128)(2,1)} %key_grad.1, ...), custom_call_target="tpu_custom_call" | custom-call | tf_op jit(solution)/shard_map/pallas_call | solution.py:319
  39.5 1.5 %shard_map.137 = (f32[128,256]{1,0:T(8,128)}, f32[128,256]{1,0:T(8,128)}, f32[128,256]{1,0:T(8,128)}, f32[128,256]{1,0:T(8,128)}, bf16[2048,256]{1,0:T(8,128)(2,1)}, /*index=5*/bf16[2048,256]{1,0:T(8,128)(2,1)}) custom-call(f32[128,256]{1,0:T(8,128)S(1)} %get-tuple-element.18.refs_0_, f32[128,256]{1,0:T(8,128)S(1)} %get-tuple-element.19.refs_1_, ...), custom_call_target="tpu_custom_call" | custom-call | tf_op jit(solution)/shard_map/pallas_call | solution.py:362
